TPU v7x, 256 devices: a whole 4x4x8 slice. The times are simulated.
256 devices in a mesh: ens: 64 (over z_lo, x, y), row: 2 (over z_hi), col: 2 (over core).
Axes of the slice: x: 4, y: 4, z: 8 (z_hi: 2, z_lo: 4; z = z_hi * 4 + z_lo), core: 2. Of those that a mesh axis runs over, the one named last changes fastest.
Arguments:
- states: float32 [128, 16, 4096], P('ens', None, ('row', 'col')), parts along dimension 0, may hold values from -4 to 4
- jacobian: bfloat16 [262144, 4096], P(('ens', 'row'), 'col'), parts along dimension 0, as said below
- step_sizes: float32 [128, 1], P('ens'), parts along dimension 0, may hold values from 0.75 to 1.5
Outputs:
- new_states: float32 [128, 16, 4096], P('ens', None, ('row', 'col')), parts along dimension 0
There are 64 independent parts, one for each index of `ens`. A program takes and returns all parts, laid end to end along the dimension named above; each array names one. Nothing has to cross between parts.
Inputs may be any that keep to these rules, and one draw needn't show every extreme that they name: `jacobian`: the diagonal lies between -40 and -1 apart from a term as small as the others, whose magnitude is at most 24 / sqrt(4096).
All inputs are finite; a program needn't handle non-finite values.
Results may differ from a plain program's by a relative error of at most 0.0083.
Values may be sent and summed in bfloat16 or wider, within the bound.
No kernel may reach another device: no remote copies, remote signals or barrier semaphores. Data moves between devices by JAX's collectives and lax.ppermute only.
A program may use at most 64 MiB of HBM per device.

v0:
```python
import jax
import jax.numpy as jnp
from jax import lax
from jax.sharding import PartitionSpec as P

BLOCKS = 12
precise = lax.Precision.HIGHEST
squarings = 10
taylor_degree = 8


def cut_along(shard, dim, length):
    before, after = (shard.shape[:dim], shard.shape[dim + 1 :])
    return jnp.moveaxis(shard.reshape(*before, length, -1, *after), dim, 0)


def sum_at_owner(shard, axis, dim):
    tiles = cut_along(shard, dim, lax.axis_size(axis))
    arrived = lax.all_to_all(tiles, axis, split_axis=0, concat_axis=0, tiled=True)
    return arrived.sum(axis=0)


def total_of_pieces(shard, axis):
    return lax.all_gather(shard, axis).sum(0)


def from_everyone(shard, axis):
    copies = jnp.broadcast_to(shard, (lax.axis_size(axis), *shard.shape))
    return lax.all_to_all(copies, axis, split_axis=0, concat_axis=0, tiled=True)


def of_everyone(shard, axis):
    everything = from_everyone(shard, axis)
    return jnp.sum(everything, axis=0)


def together(arrays, axis):
    ends = [0]
    for a in arrays:
        ends.append(ends[-1] + a.size)
    subtotal = of_everyone(jnp.concatenate([a.ravel() for a in arrays]), axis)
    return tuple((subtotal[b:e].reshape(a.shape) for a, b, e in zip(arrays, ends, ends[1:])))


def exponential(matrix):
    scaled = matrix / 2.0**squarings
    identity = jnp.eye(matrix.shape[-1], dtype=jnp.float32)
    result = jnp.broadcast_to(identity, matrix.shape)
    for degree in range(taylor_degree, 0, -1):
        result = identity + jnp.matmul(scaled, result, precision=precise) / degree
    for squaring in range(squarings):
        result = jnp.matmul(result, result, precision=precise)
    return result


def apply_jacobian(vectors, jacobian):
    rounded = vectors.astype(jnp.bfloat16)
    gathered = lax.all_gather(rounded, ("row", "col"), axis=2, tiled=True)
    tile_cols = jacobian.shape[1]
    column_piece = lax.dynamic_slice_in_dim(
        gathered, lax.axis_index("col") * tile_cols, tile_cols, 2
    )
    partial_value = jnp.einsum(
        "bcm,nm->bcn", column_piece, jacobian, preferred_element_type=jnp.float32
    )
    return sum_at_owner(partial_value, "col", 2)


def sum_projections(terms):
    return total_of_pieces(terms, ("row", "col"))


def sum_grams(terms):
    return total_of_pieces(terms, ("row", "col"))


def sum_combined(terms):
    return together((terms[0], terms[1]), ("row", "col"))


def local_gram(vectors):
    return jnp.einsum("bpn,bqn->bpq", vectors, vectors, precision=precise)


def project_block(krylov_basis, images):
    local_terms = jnp.einsum("bkn,bqn->bkq", krylov_basis, images, precision=precise)
    projection, raw_gram = sum_combined((local_terms, local_gram(images)))
    reduced = images - jnp.einsum("bkq,bkn->bqn", projection, krylov_basis, precision=precise)
    gram_matrix = raw_gram - jnp.einsum("bkp,bkq->bpq", projection, projection, precision=precise)
    return (projection, reduced, gram_matrix)


def local(states, jacobian, step_sizes):
    members = states.shape[0]
    columns = states.shape[1]
    length = states.shape[2]
    krylov = BLOCKS * columns
    forcing = apply_jacobian(states, jacobian) - states * states * states / 3.0
    root_lower = jnp.linalg.cholesky(sum_grams(local_gram(forcing)))
    leading = lax.linalg.triangular_solve(root_lower, forcing, left_side=True, lower=True)
    krylov_basis = jnp.zeros((members, krylov, length), jnp.float32)
    krylov_basis = lax.dynamic_update_slice_in_dim(krylov_basis, leading, 0, 1)
    hessenberg = jnp.zeros((members, krylov, krylov), jnp.float32)

    def arnoldi_turn(block_index, carry):
        basis_now, hess_now = carry
        start = block_index * columns
        current = lax.dynamic_slice_in_dim(basis_now, start, columns, 1)
        images = apply_jacobian(current, jacobian)
        projection, reduced, gram_matrix = project_block(basis_now, images)
        lower_factor = jnp.linalg.cholesky(gram_matrix)
        next_block = lax.linalg.triangular_solve(lower_factor, reduced, left_side=True, lower=True)
        hess_now = lax.dynamic_update_slice_in_dim(hess_now, projection, start, 2)
        sub_block = jnp.swapaxes(lower_factor, 1, 2)
        hess_now = lax.dynamic_update_slice(
            hess_now, sub_block, (jnp.int32(0), start + columns, start)
        )
        basis_now = lax.dynamic_update_slice_in_dim(basis_now, next_block, start + columns, 1)
        return (basis_now, hess_now)

    krylov_basis, hessenberg = lax.fori_loop(
        0, BLOCKS - 1, arnoldi_turn, (krylov_basis, hessenberg)
    )
    last_start = (BLOCKS - 1) * columns
    last_block = krylov_basis[:, last_start : last_start + columns]
    last_images = apply_jacobian(last_block, jacobian)
    last_column = sum_projections(
        jnp.einsum("bkn,bqn->bkq", krylov_basis, last_images, precision=precise)
    )
    hessenberg = hessenberg.at[:, :, last_start : last_start + columns].set(last_column)
    step_size = step_sizes[:, 0][:, None, None]
    augmented = jnp.zeros((members, krylov + columns, krylov + columns), jnp.float32)
    augmented = augmented.at[:, :krylov, :krylov].set(step_size * hessenberg)
    augmented = augmented.at[:, :columns, krylov:].set(step_size * jnp.swapaxes(root_lower, 1, 2))
    exponent = exponential(augmented)
    phi_block = exponent[:, :krylov, krylov:]
    states = states + jnp.einsum("bkq,bkn->bqn", phi_block, krylov_basis, precision=precise)
    return states


def solution(mesh):
    placed = (P("ens", None, ("row", "col")), P(("ens", "row"), "col"), P("ens", None))
    return jax.shard_map(
        local, mesh=mesh, in_specs=placed, out_specs=P("ens", None, ("row", "col")), check_vma=False
    )
```

profile of v0, /device:TPU:1, one launch (start us, length us, event | category | flops | bytes accessed | tf_op | source)
XLA Modules:
  0.0 581.9 jit_solution(12738345656807627171)
XLA Ops:
  0.9 12.9 %all_gather.28 = bf16[2,16,4096]{2,1,0:T(8,128)(2,1)S(1)} all-gather(bf16[2,16,1024]{2,1,0:T(8,128)(2,1)S(1)} %convert_element_type.38), channel_id=1, replica_groups=mesh['ens'=64,'row'=2,'col'=2] {'row','col'}, dimensions={2}, use_global_device_ids=true | all-gather | bytes 327680 | tf_op jit(solution)/shard_map/all_gather | solution.py:58
  23.9 9.3 %all-gather = f32[8,16,16]{2,1,0:T(8,128)S(1)} all-gather(f32[2,16,16]{2,1,0:T(8,128)S(1)} %fusion.45), channel_id=2, replica_groups=mesh['ens'=64,'row'=2,'col'=2] {'row','col'}, dimensions={0}, use_global_device_ids=true | all-gather | bytes 10240 | tf_op jit(solution)/shard_map/all_gather | solution.py:24
  39.6 487.2 %while.20 = (s32[]{:T(128)}, f32[2,192,1024]{2,1,0:T(8,128)S(1)}, f32[2,192,192]{1,2,0:T(8,128)S(1)}, bf16[2048,2048]{1,0:T(8,128)(2,1)}, s32[]{:T(128)}, /*inde...) while((s32[]{:T(128)}, f32[2,192,1024]{2,1,0:T(8,128)S(1)}, ...), condition=%wide.region_7.10_spmd, body=%wide.region_4.9_spmd.sunk | while | flops 433289760 | bytes 15701595 | solution.py:121
  39.6 9.9 %all_gather.35 = bf16[2,16,4096]{2,1,0:T(8,128)(2,1)S(1)} all-gather(bf16[2,16,1024]{2,1,0:T(8,128)(2,1)S(1)} %dynamic-slice_convert_fusion.2), channel_id=1, replica_groups=mesh['ens'=64,'row'=2,'col'=2] {'row','col'}, dimensions={2}, use_global_device_ids=true | all-gather | bytes 327680 | tf_op jit(solution)/shard_map/while/body/eval_jaxpr/all_gather | solution.py:58
  85.5 10.6 %all_gather.35 = bf16[2,16,4096]{2,1,0:T(8,128)(2,1)S(1)} all-gather(bf16[2,16,1024]{2,1,0:T(8,128)(2,1)S(1)} %dynamic-slice_convert_fusion.2), channel_id=1, replica_groups=mesh['ens'=64,'row'=2,'col'=2] {'row','col'}, dimensions={2}, use_global_device_ids=true | all-gather | bytes 327680 | tf_op jit(solution)/shard_map/while/body/eval_jaxpr/all_gather | solution.py:58
  128.7 11.8 %all_gather.35 = bf16[2,16,4096]{2,1,0:T(8,128)(2,1)S(1)} all-gather(bf16[2,16,1024]{2,1,0:T(8,128)(2,1)S(1)} %dynamic-slice_convert_fusion.2), channel_id=1, replica_groups=mesh['ens'=64,'row'=2,'col'=2] {'row','col'}, dimensions={2}, use_global_device_ids=true | all-gather | bytes 327680 | tf_op jit(solution)/shard_map/while/body/eval_jaxpr/all_gather | solution.py:58
  156.7 7.4 %all-to-all-done.1 = f32[4,1,6656]{2,1,0:T(1,128)S(1)} async-done(((f32[4,1,6656]{2,1,0:T(1,128)}), f32[4,1,6656]{2,1,0:T(1,128)S(1)}, u32[]{:S(2)}, u32[]{:S(2)}) %all-to-all-start.1) | async-done | bytes 106528 | tf_op jit(solution)/shard_map/while/body/eval_jaxpr/all_to_all | solution.py:29
  173.2 11.6 %all_gather.35 = bf16[2,16,4096]{2,1,0:T(8,128)(2,1)S(1)} all-gather(bf16[2,16,1024]{2,1,0:T(8,128)(2,1)S(1)} %dynamic-slice_convert_fusion.2), channel_id=1, replica_groups=mesh['ens'=64,'row'=2,'col'=2] {'row','col'}, dimensions={2}, use_global_device_ids=true | all-gather | bytes 327680 | tf_op jit(solution)/shard_map/while/body/eval_jaxpr/all_gather | solution.py:58
  201.0 7.4 %all-to-all-done.1 = f32[4,1,6656]{2,1,0:T(1,128)S(1)} async-done(((f32[4,1,6656]{2,1,0:T(1,128)}), f32[4,1,6656]{2,1,0:T(1,128)S(1)}, u32[]{:S(2)}, u32[]{:S(2)}) %all-to-all-start.1) | async-done | bytes 106528 | tf_op jit(solution)/shard_map/while/body/eval_jaxpr/all_to_all | solution.py:29
  217.6 11.6 %all_gather.35 = bf16[2,16,4096]{2,1,0:T(8,128)(2,1)S(1)} all-gather(bf16[2,16,1024]{2,1,0:T(8,128)(2,1)S(1)} %dynamic-slice_convert_fusion.2), channel_id=1, replica_groups=mesh['ens'=64,'row'=2,'col'=2] {'row','col'}, dimensions={2}, use_global_device_ids=true | all-gather | bytes 327680 | tf_op jit(solution)/shard_map/while/body/eval_jaxpr/all_gather | solution.py:58
  261.9 11.6 %all_gather.35 = bf16[2,16,4096]{2,1,0:T(8,128)(2,1)S(1)} all-gather(bf16[2,16,1024]{2,1,0:T(8,128)(2,1)S(1)} %dynamic-slice_convert_fusion.2), channel_id=1, replica_groups=mesh['ens'=64,'row'=2,'col'=2] {'row','col'}, dimensions={2}, use_global_device_ids=true | all-gather | bytes 327680 | tf_op jit(solution)/shard_map/while/body/eval_jaxpr/all_gather | solution.py:58
  289.7 7.4 %all-to-all-done.1 = f32[4,1,6656]{2,1,0:T(1,128)S(1)} async-done(((f32[4,1,6656]{2,1,0:T(1,128)}), f32[4,1,6656]{2,1,0:T(1,128)S(1)}, u32[]{:S(2)}, u32[]{:S(2)}) %all-to-all-start.1) | async-done | bytes 106528 | tf_op jit(solution)/shard_map/while/body/eval_jaxpr/all_to_all | solution.py:29
  306.3 11.6 %all_gather.35 = bf16[2,16,4096]{2,1,0:T(8,128)(2,1)S(1)} all-gather(bf16[2,16,1024]{2,1,0:T(8,128)(2,1)S(1)} %dynamic-slice_convert_fusion.2), channel_id=1, replica_groups=mesh['ens'=64,'row'=2,'col'=2] {'row','col'}, dimensions={2}, use_global_device_ids=true | all-gather | bytes 327680 | tf_op jit(solution)/shard_map/while/body/eval_jaxpr/all_gather | solution.py:58
  334.0 7.4 %all-to-all-done.1 = f32[4,1,6656]{2,1,0:T(1,128)S(1)} async-done(((f32[4,1,6656]{2,1,0:T(1,128)}), f32[4,1,6656]{2,1,0:T(1,128)S(1)}, u32[]{:S(2)}, u32[]{:S(2)}) %all-to-all-start.1) | async-done | bytes 106528 | tf_op jit(solution)/shard_map/while/body/eval_jaxpr/all_to_all | solution.py:29
  350.6 11.6 %all_gather.35 = bf16[2,16,4096]{2,1,0:T(8,128)(2,1)S(1)} all-gather(bf16[2,16,1024]{2,1,0:T(8,128)(2,1)S(1)} %dynamic-slice_convert_fusion.2), channel_id=1, replica_groups=mesh['ens'=64,'row'=2,'col'=2] {'row','col'}, dimensions={2}, use_global_device_ids=true | all-gather | bytes 327680 | tf_op jit(solution)/shard_map/while/body/eval_jaxpr/all_gather | solution.py:58
  378.4 7.4 %all-to-all-done.1 = f32[4,1,6656]{2,1,0:T(1,128)S(1)} async-done(((f32[4,1,6656]{2,1,0:T(1,128)}), f32[4,1,6656]{2,1,0:T(1,128)S(1)}, u32[]{:S(2)}, u32[]{:S(2)}) %all-to-all-start.1) | async-done | bytes 106528 | tf_op jit(solution)/shard_map/while/body/eval_jaxpr/all_to_all | solution.py:29
  394.3 11.6 %all_gather.35 = bf16[2,16,4096]{2,1,0:T(8,128)(2,1)S(1)} all-gather(bf16[2,16,1024]{2,1,0:T(8,128)(2,1)S(1)} %dynamic-slice_convert_fusion.2), channel_id=1, replica_groups=mesh['ens'=64,'row'=2,'col'=2] {'row','col'}, dimensions={2}, use_global_device_ids=true | all-gather | bytes 327680 | tf_op jit(solution)/shard_map/while/body/eval_jaxpr/all_gather | solution.py:58
  422.0 7.4 %all-to-all-done.1 = f32[4,1,6656]{2,1,0:T(1,128)S(1)} async-done(((f32[4,1,6656]{2,1,0:T(1,128)}), f32[4,1,6656]{2,1,0:T(1,128)S(1)}, u32[]{:S(2)}, u32[]{:S(2)}) %all-to-all-start.1) | async-done | bytes 106528 | tf_op jit(solution)/shard_map/while/body/eval_jaxpr/all_to_all | solution.py:29
  438.4 11.6 %all_gather.35 = bf16[2,16,4096]{2,1,0:T(8,128)(2,1)S(1)} all-gather(bf16[2,16,1024]{2,1,0:T(8,128)(2,1)S(1)} %dynamic-slice_convert_fusion.2), channel_id=1, replica_groups=mesh['ens'=64,'row'=2,'col'=2] {'row','col'}, dimensions={2}, use_global_device_ids=true | all-gather | bytes 327680 | tf_op jit(solution)/shard_map/while/body/eval_jaxpr/all_gather | solution.py:58
  466.2 7.4 %all-to-all-done.1 = f32[4,1,6656]{2,1,0:T(1,128)S(1)} async-done(((f32[4,1,6656]{2,1,0:T(1,128)}), f32[4,1,6656]{2,1,0:T(1,128)S(1)}, u32[]{:S(2)}, u32[]{:S(2)}) %all-to-all-start.1) | async-done | bytes 106528 | tf_op jit(solution)/shard_map/while/body/eval_jaxpr/all_to_all | solution.py:29
  482.6 11.6 %all_gather.35 = bf16[2,16,4096]{2,1,0:T(8,128)(2,1)S(1)} all-gather(bf16[2,16,1024]{2,1,0:T(8,128)(2,1)S(1)} %dynamic-slice_convert_fusion.2), channel_id=1, replica_groups=mesh['ens'=64,'row'=2,'col'=2] {'row','col'}, dimensions={2}, use_global_device_ids=true | all-gather | bytes 327680 | tf_op jit(solution)/shard_map/while/body/eval_jaxpr/all_gather | solution.py:58
  510.4 7.4 %all-to-all-done.1 = f32[4,1,6656]{2,1,0:T(1,128)S(1)} async-done(((f32[4,1,6656]{2,1,0:T(1,128)}), f32[4,1,6656]{2,1,0:T(1,128)S(1)}, u32[]{:S(2)}, u32[]{:S(2)}) %all-to-all-start.1) | async-done | bytes 106528 | tf_op jit(solution)/shard_map/while/body/eval_jaxpr/all_to_all | solution.py:29
  526.8 11.8 %all_gather.31 = bf16[2,16,4096]{2,1,0:T(8,128)(2,1)S(1)} all-gather(bf16[2,16,1024]{2,1,0:T(8,128)(2,1)S(1)} %slice.135), channel_id=1, replica_groups=mesh['ens'=64,'row'=2,'col'=2] {'row','col'}, dimensions={2}, use_global_device_ids=true | all-gather | bytes 327680 | tf_op jit(solution)/shard_map/all_gather | solution.py:58
  551.7 9.6 %all-gather.1 = f32[8,192,16]{1,2,0:T(8,128)S(1)} all-gather(f32[2,192,16]{1,2,0:T(8,128)S(1)} %fusion.63), channel_id=3, replica_groups=mesh['ens'=64,'row'=2,'col'=2] {'row','col'}, dimensions={0}, use_global_device_ids=true | all-gather | bytes 122880 | tf_op jit(solution)/shard_map/all_gather | solution.py:24
  (438 shorter events, 352.3 us)
Async XLA Ops:
  13.8 9.8 %copy-start = (f32[2,16,1024]{2,1,0:T(8,128)S(1)}, f32[2,16,1024]{2,1,0:T(8,128)}, u32[]{:S(2)}) copy-start(f32[2,16,1024]{2,1,0:T(8,128)} %param.14) | copy-start | bytes 393220
  62.0 14.3 %all-to-all-start.1 = ((f32[4,1,6656]{2,1,0:T(1,128)}), f32[4,1,6656]{2,1,0:T(1,128)S(1)}, u32[]{:S(2)}, u32[]{:S(2)}) async-start(f32[4,1,6656]{2,1,0:T(1,128)} %broadcast_in_dim.16), calls=%async_computation.1 | async-start | bytes 212992 | tf_op jit(solution)/shard_map/while/body/eval_jaxpr/all_to_all | solution.py:29
  108.6 10.9 %all-to-all-start.1 = ((f32[4,1,6656]{2,1,0:T(1,128)}), f32[4,1,6656]{2,1,0:T(1,128)S(1)}, u32[]{:S(2)}, u32[]{:S(2)}) async-start(f32[4,1,6656]{2,1,0:T(1,128)} %broadcast_in_dim.16), calls=%async_computation.1 | async-start | bytes 212992 | tf_op jit(solution)/shard_map/while/body/eval_jaxpr/all_to_all | solution.py:29
  153.0 11.0 %all-to-all-start.1 = ((f32[4,1,6656]{2,1,0:T(1,128)}), f32[4,1,6656]{2,1,0:T(1,128)S(1)}, u32[]{:S(2)}, u32[]{:S(2)}) async-start(f32[4,1,6656]{2,1,0:T(1,128)} %broadcast_in_dim.16), calls=%async_computation.1 | async-start | bytes 212992 | tf_op jit(solution)/shard_map/while/body/eval_jaxpr/all_to_all | solution.py:29
  197.4 11.0 %all-to-all-start.1 = ((f32[4,1,6656]{2,1,0:T(1,128)}), f32[4,1,6656]{2,1,0:T(1,128)S(1)}, u32[]{:S(2)}, u32[]{:S(2)}) async-start(f32[4,1,6656]{2,1,0:T(1,128)} %broadcast_in_dim.16), calls=%async_computation.1 | async-start | bytes 212992 | tf_op jit(solution)/shard_map/while/body/eval_jaxpr/all_to_all | solution.py:29
  241.7 11.0 %all-to-all-start.1 = ((f32[4,1,6656]{2,1,0:T(1,128)}), f32[4,1,6656]{2,1,0:T(1,128)S(1)}, u32[]{:S(2)}, u32[]{:S(2)}) async-start(f32[4,1,6656]{2,1,0:T(1,128)} %broadcast_in_dim.16), calls=%async_computation.1 | async-start | bytes 212992 | tf_op jit(solution)/shard_map/while/body/eval_jaxpr/all_to_all | solution.py:29
  286.0 11.0 %all-to-all-start.1 = ((f32[4,1,6656]{2,1,0:T(1,128)}), f32[4,1,6656]{2,1,0:T(1,128)S(1)}, u32[]{:S(2)}, u32[]{:S(2)}) async-start(f32[4,1,6656]{2,1,0:T(1,128)} %broadcast_in_dim.16), calls=%async_computation.1 | async-start | bytes 212992 | tf_op jit(solution)/shard_map/while/body/eval_jaxpr/all_to_all | solution.py:29
  330.4 11.0 %all-to-all-start.1 = ((f32[4,1,6656]{2,1,0:T(1,128)}), f32[4,1,6656]{2,1,0:T(1,128)S(1)}, u32[]{:S(2)}, u32[]{:S(2)}) async-start(f32[4,1,6656]{2,1,0:T(1,128)} %broadcast_in_dim.16), calls=%async_computation.1 | async-start | bytes 212992 | tf_op jit(solution)/shard_map/while/body/eval_jaxpr/all_to_all | solution.py:29
  374.7 11.0 %all-to-all-start.1 = ((f32[4,1,6656]{2,1,0:T(1,128)}), f32[4,1,6656]{2,1,0:T(1,128)S(1)}, u32[]{:S(2)}, u32[]{:S(2)}) async-start(f32[4,1,6656]{2,1,0:T(1,128)} %broadcast_in_dim.16), calls=%async_computation.1 | async-start | bytes 212992 | tf_op jit(solution)/shard_map/while/body/eval_jaxpr/all_to_all | solution.py:29
  418.4 11.0 %all-to-all-start.1 = ((f32[4,1,6656]{2,1,0:T(1,128)}), f32[4,1,6656]{2,1,0:T(1,128)S(1)}, u32[]{:S(2)}, u32[]{:S(2)}) async-start(f32[4,1,6656]{2,1,0:T(1,128)} %broadcast_in_dim.16), calls=%async_computation.1 | async-start | bytes 212992 | tf_op jit(solution)/shard_map/while/body/eval_jaxpr/all_to_all | solution.py:29
  462.6 11.0 %all-to-all-start.1 = ((f32[4,1,6656]{2,1,0:T(1,128)}), f32[4,1,6656]{2,1,0:T(1,128)S(1)}, u32[]{:S(2)}, u32[]{:S(2)}) async-start(f32[4,1,6656]{2,1,0:T(1,128)} %broadcast_in_dim.16), calls=%async_computation.1 | async-start | bytes 212992 | tf_op jit(solution)/shard_map/while/body/eval_jaxpr/all_to_all | solution.py:29
  506.8 11.0 %all-to-all-start.1 = ((f32[4,1,6656]{2,1,0:T(1,128)}), f32[4,1,6656]{2,1,0:T(1,128)S(1)}, u32[]{:S(2)}, u32[]{:S(2)}) async-start(f32[4,1,6656]{2,1,0:T(1,128)} %broadcast_in_dim.16), calls=%async_computation.1 | async-start | bytes 212992 | tf_op jit(solution)/shard_map/while/body/eval_jaxpr/all_to_all | solution.py:29
  545.3 16.6 %copy-start.1 = (f32[2,1]{0,1:T(1,128)S(1)}, f32[2,1]{0,1:T(1,128)}, u32[]{:S(2)}) copy-start(f32[2,1]{0,1:T(1,128)} %param.16) | copy-start | bytes 28
  545.3 4.9 all-to-all-start.3
  550.2 11.8 %copy-start.2 = (s32[3]{0:T(128)S(1)}, s32[3]{0:T(128)}, u32[]{:S(2)}) copy-start(s32[3]{0:T(128)} %constant.233.clone.1) | copy-start | bytes 40
where the time goes:
time: 584 us; the launch traced here: 582 us
  blocking collectives  214 us (37%)
  matrix products  131 us (22%)
  waiting for transfers between devices  82.1 us (14%)
  other arithmetic  72.9 us (12%)
  starting transfers between devices  47.2 us (8%)
  local copies, waits for them, and re-layouts  32.8 us (6%)
    all_gather x13, blocking collectives, apply_jacobian(): gathered = lax.all_gather(rounded, ('row', 'col'), axis=2, tiled=True)  150 us
    all_to_all x11, waiting for transfers between devices, from_everyone(): return lax.all_to_all(copies, axis, split_axis=0, concat_axis=0, tiled=True)  80.9 us
    dot_general x13, matrix products, apply_jacobian(): jnp.einsum('bcm,nm->bcn', column_piece, jacobian, preferred_element_type=...  77.5 us
    all_to_all x12, blocking collectives, sum_at_owner(): lax.all_to_all(tiles, axis, split_axis=0, concat_axis=0, tiled=True)  44.9 us
    all_to_all x11, starting transfers between devices, from_everyone(): return lax.all_to_all(copies, axis, split_axis=0, concat_axis=0, tiled=True)  43.5 us
    another operation x44, other arithmetic, arnoldi_turn(): lower_factor = jnp.linalg.cholesky(gram_matrix)  34 us
    another operation x22, other arithmetic, arnoldi_turn(): lax.linalg.triangular_solve(lower_factor, reduced, left_side=True, lower=...  27.2 us
    all_gather x2, blocking collectives, total_of_pieces(): return lax.all_gather(shard, axis).sum(0)  18.9 us
  transfers between devices with their start and end apart: 12, of which 12 were waited for; matrix products, arithmetic and copies ran while one was open for 0% of the time, Pallas kernels for 0%

commit v1 on v0

--- a/solution.py
+++ b/solution.py
@@ -55,7 +55,10 @@
 
 def apply_jacobian(vectors, jacobian):
     rounded = vectors.astype(jnp.bfloat16)
-    gathered = lax.all_gather(rounded, ("row", "col"), axis=2, tiled=True)
+    gathered = jnp.concatenate(
+        lax.all_to_all(jnp.stack([rounded] * lax.axis_size(("row", "col"))), ("row", "col"), 0, 0),
+        axis=2,
+    )
     tile_cols = jacobian.shape[1]
     column_piece = lax.dynamic_slice_in_dim(
         gathered, lax.axis_index("col") * tile_cols, tile_cols, 2

time: 584 us -> 661 us (1.13)
  waiting for transfers between devices: 82.1 us -> 197 us
  blocking collectives: 214 us -> 111 us
  starting transfers between devices: 47.2 us -> 101 us
  local copies, waits for them, and re-layouts: 32.8 us -> 41.6 us
    all_gather x13 -> x0, blocking collectives: 150 us -> none  [apply_jacobian(): gathered = lax.all_gather(rounded, ('row', 'col'), axis=2, tiled=True)]
    all_to_all x1 -> x13, waiting for transfers between devices: 1.18 us -> 116 us  [apply_jacobian(): lax.all_to_all(jnp.stack([rounded] * lax.axis_size(('row', 'col'))), ('ro...]
    all_to_all x1 -> x13, starting transfers between devices: 3.73 us -> 61.3 us  [apply_jacobian(): lax.all_to_all(jnp.stack([rounded] * lax.axis_size(('row', 'col'))), ('ro...]
    all_to_all x12 -> x13, blocking collectives: 44.9 us -> 92 us  [sum_at_owner(): lax.all_to_all(tiles, axis, split_axis=0, concat_axis=0, tiled=True)]
    another operation x1 -> x14, local copies, waits for them, and re-layouts: 0.59 us -> 9.94 us  [the longest x13 9.35 us: apply_jacobian(): jnp.stack([rounded] * lax.axis_size(('row', 'col')))]
  transfers between devices with their start and end apart: 12 -> 24, of which waited for: 12 -> 24; matrix products, arithmetic and copies ran while one was open for 0% -> 0% of each run, Pallas kernels for 0% -> 0%
where the time goes in v1:
time: 661 us; the launch traced here: 658 us
  waiting for transfers between devices  197 us (30%)
  matrix products  132 us (20%)
  blocking collectives  111 us (17%)
  starting transfers between devices  101 us (15%)
  other arithmetic  72.9 us (11%)
  local copies, waits for them, and re-layouts  41.6 us (6%)
    all_to_all x13, waiting for transfers between devices, apply_jacobian(): lax.all_to_all(jnp.stack([rounded] * lax.axis_size(('row', 'col'))), ('ro...  116 us
    all_to_all x13, blocking collectives, sum_at_owner(): lax.all_to_all(tiles, axis, split_axis=0, concat_axis=0, tiled=True)  92 us
    all_to_all x11, waiting for transfers between devices, from_everyone(): return lax.all_to_all(copies, axis, split_axis=0, concat_axis=0, tiled=True)  81 us
    dot_general x13, matrix products, apply_jacobian(): jnp.einsum('bcm,nm->bcn', column_piece, jacobian, preferred_element_type=...  77.6 us
    all_to_all x13, starting transfers between devices, apply_jacobian(): lax.all_to_all(jnp.stack([rounded] * lax.axis_size(('row', 'col'))), ('ro...  61.3 us
    all_to_all x11, starting transfers between devices, from_everyone(): return lax.all_to_all(copies, axis, split_axis=0, concat_axis=0, tiled=True)  40 us
    another operation x44, other arithmetic, arnoldi_turn(): lower_factor = jnp.linalg.cholesky(gram_matrix)  34 us
    another operation x22, other arithmetic, arnoldi_turn(): lax.linalg.triangular_solve(lower_factor, reduced, left_side=True, lower=...  27.2 us
  transfers between devices with their start and end apart: 24, of which 24 were waited for; matrix products, arithmetic and copies ran while one was open for 0% of the time, Pallas kernels for 0%

profile of v1, /device:TPU:1, one launch (start us, length us, event | category | flops | bytes accessed | tf_op | source)
XLA Modules:
  0.0 657.5 jit_solution(11474658649161881134)
XLA Ops:
  1.6 9.9 %all-to-all-start.3 = ((bf16[4,2,16,1024]{3,2,1,0:T(8,128)(2,1)}), bf16[4,2,16,1024]{3,2,1,0:T(8,128)(2,1)S(1)}, u32[]{:S(2)}, u32[]{:S(2)}) async-start(bf16[4,2,16,1024]{3,2,1,0:T(8,128)(2,1)} %stack.15), calls=%async_computation.3 | async-start | bytes 524288 | tf_op jit(solution)/shard_map/all_to_all | solution.py:59
  11.6 8.9 %all-to-all-done.3 = bf16[4,2,16,1024]{3,2,1,0:T(8,128)(2,1)S(1)} async-done(((bf16[4,2,16,1024]{3,2,1,0:T(8,128)(2,1)}), bf16[4,2,16,1024]{3,2,1,0:T(8,128)(2,1)S(1)}, u32[]{:S(2)}, u32[]{:S(2)}) %all-to-all-start.3) | async-done | bytes 262176 | tf_op jit(solution)/shard_map/all_to_all | solution.py:59
  31.6 9.3 %all-gather = f32[8,16,16]{2,1,0:T(8,128)S(1)} all-gather(f32[2,16,16]{2,1,0:T(8,128)S(1)} %fusion.45), channel_id=2, replica_groups=mesh['ens'=64,'row'=2,'col'=2] {'row','col'}, dimensions={0}, use_global_device_ids=true | all-gather | bytes 10240 | tf_op jit(solution)/shard_map/all_gather | solution.py:24
  47.2 552.0 %while.20 = (s32[]{:T(128)}, f32[2,192,1024]{2,1,0:T(8,128)S(1)}, f32[2,192,192]{1,2,0:T(8,128)S(1)}, bf16[2048,2048]{1,0:T(8,128)(2,1)}, s32[]{:T(128)}, /*inde...) while((s32[]{:T(128)}, f32[2,192,1024]{2,1,0:T(8,128)S(1)}, ...), condition=%wide.region_7.10_spmd, body=%wide.region_4.9_spmd.sunk | while | flops 433289760 | bytes 17012348 | solution.py:124
  51.5 9.0 %all-to-all-done = bf16[4,2,16,1024]{3,2,1,0:T(8,128)(2,1)S(1)} async-done(((bf16[4,2,16,1024]{3,2,1,0:T(8,128)(2,1)}), bf16[4,2,16,1024]{3,2,1,0:T(8,128)(2,1)S(1)}, u32[]{:S(2)}, u32[]{:S(2)}) %all-to-all-start) | async-done | bytes 262176 | tf_op jit(solution)/shard_map/while/body/eval_jaxpr/all_to_all | solution.py:59
  101.9 9.0 %all-to-all-done = bf16[4,2,16,1024]{3,2,1,0:T(8,128)(2,1)S(1)} async-done(((bf16[4,2,16,1024]{3,2,1,0:T(8,128)(2,1)}), bf16[4,2,16,1024]{3,2,1,0:T(8,128)(2,1)S(1)}, u32[]{:S(2)}, u32[]{:S(2)}) %all-to-all-start) | async-done | bytes 262176 | tf_op jit(solution)/shard_map/while/body/eval_jaxpr/all_to_all | solution.py:59
  130.7 7.4 %all-to-all-done.2 = f32[4,1,6656]{2,1,0:T(1,128)S(1)} async-done(((f32[4,1,6656]{2,1,0:T(1,128)}), f32[4,1,6656]{2,1,0:T(1,128)S(1)}, u32[]{:S(2)}, u32[]{:S(2)}) %all-to-all-start.2) | async-done | bytes 106528 | tf_op jit(solution)/shard_map/while/body/eval_jaxpr/all_to_all | solution.py:29
  152.3 9.0 %all-to-all-done = bf16[4,2,16,1024]{3,2,1,0:T(8,128)(2,1)S(1)} async-done(((bf16[4,2,16,1024]{3,2,1,0:T(8,128)(2,1)}), bf16[4,2,16,1024]{3,2,1,0:T(8,128)(2,1)S(1)}, u32[]{:S(2)}, u32[]{:S(2)}) %all-to-all-start) | async-done | bytes 262176 | tf_op jit(solution)/shard_map/while/body/eval_jaxpr/all_to_all | solution.py:59
  181.0 7.4 %all-to-all-done.2 = f32[4,1,6656]{2,1,0:T(1,128)S(1)} async-done(((f32[4,1,6656]{2,1,0:T(1,128)}), f32[4,1,6656]{2,1,0:T(1,128)S(1)}, u32[]{:S(2)}, u32[]{:S(2)}) %all-to-all-start.2) | async-done | bytes 106528 | tf_op jit(solution)/shard_map/while/body/eval_jaxpr/all_to_all | solution.py:29
  202.6 9.0 %all-to-all-done = bf16[4,2,16,1024]{3,2,1,0:T(8,128)(2,1)S(1)} async-done(((bf16[4,2,16,1024]{3,2,1,0:T(8,128)(2,1)}), bf16[4,2,16,1024]{3,2,1,0:T(8,128)(2,1)S(1)}, u32[]{:S(2)}, u32[]{:S(2)}) %all-to-all-start) | async-done | bytes 262176 | tf_op jit(solution)/shard_map/while/body/eval_jaxpr/all_to_all | solution.py:59
  253.0 9.0 %all-to-all-done = bf16[4,2,16,1024]{3,2,1,0:T(8,128)(2,1)S(1)} async-done(((bf16[4,2,16,1024]{3,2,1,0:T(8,128)(2,1)}), bf16[4,2,16,1024]{3,2,1,0:T(8,128)(2,1)S(1)}, u32[]{:S(2)}, u32[]{:S(2)}) %all-to-all-start) | async-done | bytes 262176 | tf_op jit(solution)/shard_map/while/body/eval_jaxpr/all_to_all | solution.py:59
  281.8 7.4 %all-to-all-done.2 = f32[4,1,6656]{2,1,0:T(1,128)S(1)} async-done(((f32[4,1,6656]{2,1,0:T(1,128)}), f32[4,1,6656]{2,1,0:T(1,128)S(1)}, u32[]{:S(2)}, u32[]{:S(2)}) %all-to-all-start.2) | async-done | bytes 106528 | tf_op jit(solution)/shard_map/while/body/eval_jaxpr/all_to_all | solution.py:29
  303.4 9.0 %all-to-all-done = bf16[4,2,16,1024]{3,2,1,0:T(8,128)(2,1)S(1)} async-done(((bf16[4,2,16,1024]{3,2,1,0:T(8,128)(2,1)}), bf16[4,2,16,1024]{3,2,1,0:T(8,128)(2,1)S(1)}, u32[]{:S(2)}, u32[]{:S(2)}) %all-to-all-start) | async-done | bytes 262176 | tf_op jit(solution)/shard_map/while/body/eval_jaxpr/all_to_all | solution.py:59
  332.1 7.4 %all-to-all-done.2 = f32[4,1,6656]{2,1,0:T(1,128)S(1)} async-done(((f32[4,1,6656]{2,1,0:T(1,128)}), f32[4,1,6656]{2,1,0:T(1,128)S(1)}, u32[]{:S(2)}, u32[]{:S(2)}) %all-to-all-start.2) | async-done | bytes 106528 | tf_op jit(solution)/shard_map/while/body/eval_jaxpr/all_to_all | solution.py:29
  353.7 9.0 %all-to-all-done = bf16[4,2,16,1024]{3,2,1,0:T(8,128)(2,1)S(1)} async-done(((bf16[4,2,16,1024]{3,2,1,0:T(8,128)(2,1)}), bf16[4,2,16,1024]{3,2,1,0:T(8,128)(2,1)S(1)}, u32[]{:S(2)}, u32[]{:S(2)}) %all-to-all-start) | async-done | bytes 262176 | tf_op jit(solution)/shard_map/while/body/eval_jaxpr/all_to_all | solution.py:59
  404.1 9.0 %all-to-all-done = bf16[4,2,16,1024]{3,2,1,0:T(8,128)(2,1)S(1)} async-done(((bf16[4,2,16,1024]{3,2,1,0:T(8,128)(2,1)}), bf16[4,2,16,1024]{3,2,1,0:T(8,128)(2,1)S(1)}, u32[]{:S(2)}, u32[]{:S(2)}) %all-to-all-start) | async-done | bytes 262176 | tf_op jit(solution)/shard_map/while/body/eval_jaxpr/all_to_all | solution.py:59
  432.9 7.4 %all-to-all-done.2 = f32[4,1,6656]{2,1,0:T(1,128)S(1)} async-done(((f32[4,1,6656]{2,1,0:T(1,128)}), f32[4,1,6656]{2,1,0:T(1,128)S(1)}, u32[]{:S(2)}, u32[]{:S(2)}) %all-to-all-start.2) | async-done | bytes 106528 | tf_op jit(solution)/shard_map/while/body/eval_jaxpr/all_to_all | solution.py:29
  453.8 9.0 %all-to-all-done = bf16[4,2,16,1024]{3,2,1,0:T(8,128)(2,1)S(1)} async-done(((bf16[4,2,16,1024]{3,2,1,0:T(8,128)(2,1)}), bf16[4,2,16,1024]{3,2,1,0:T(8,128)(2,1)S(1)}, u32[]{:S(2)}, u32[]{:S(2)}) %all-to-all-start) | async-done | bytes 262176 | tf_op jit(solution)/shard_map/while/body/eval_jaxpr/all_to_all | solution.py:59
  504.0 9.0 %all-to-all-done = bf16[4,2,16,1024]{3,2,1,0:T(8,128)(2,1)S(1)} async-done(((bf16[4,2,16,1024]{3,2,1,0:T(8,128)(2,1)}), bf16[4,2,16,1024]{3,2,1,0:T(8,128)(2,1)S(1)}, u32[]{:S(2)}, u32[]{:S(2)}) %all-to-all-start) | async-done | bytes 262176 | tf_op jit(solution)/shard_map/while/body/eval_jaxpr/all_to_all | solution.py:59
  532.7 7.4 %all-to-all-done.2 = f32[4,1,6656]{2,1,0:T(1,128)S(1)} async-done(((f32[4,1,6656]{2,1,0:T(1,128)}), f32[4,1,6656]{2,1,0:T(1,128)S(1)}, u32[]{:S(2)}, u32[]{:S(2)}) %all-to-all-start.2) | async-done | bytes 106528 | tf_op jit(solution)/shard_map/while/body/eval_jaxpr/all_to_all | solution.py:29
  554.2 9.0 %all-to-all-done = bf16[4,2,16,1024]{3,2,1,0:T(8,128)(2,1)S(1)} async-done(((bf16[4,2,16,1024]{3,2,1,0:T(8,128)(2,1)}), bf16[4,2,16,1024]{3,2,1,0:T(8,128)(2,1)S(1)}, u32[]{:S(2)}, u32[]{:S(2)}) %all-to-all-start) | async-done | bytes 262176 | tf_op jit(solution)/shard_map/while/body/eval_jaxpr/all_to_all | solution.py:59
  582.9 7.4 %all-to-all-done.2 = f32[4,1,6656]{2,1,0:T(1,128)S(1)} async-done(((f32[4,1,6656]{2,1,0:T(1,128)}), f32[4,1,6656]{2,1,0:T(1,128)S(1)}, u32[]{:S(2)}, u32[]{:S(2)}) %all-to-all-start.2) | async-done | bytes 106528 | tf_op jit(solution)/shard_map/while/body/eval_jaxpr/all_to_all | solution.py:29
  605.7 7.7 %all-to-all-done.5 = bf16[4,2,16,1024]{3,2,1,0:T(8,128)(2,1)S(1)} async-done(((bf16[4,2,16,1024]{3,2,1,0:T(8,128)(2,1)}), bf16[4,2,16,1024]{3,2,1,0:T(8,128)(2,1)S(1)}, u32[]{:S(2)}, u32[]{:S(2)}) %all-to-all-start.5) | async-done | bytes 262176 | tf_op jit(solution)/shard_map/all_to_all | solution.py:59
  628.2 10.1 %all-gather.1 = f32[8,192,16]{1,2,0:T(8,128)S(1)} all-gather(f32[2,192,16]{1,2,0:T(8,128)S(1)} %fusion.63), channel_id=3, replica_groups=mesh['ens'=64,'row'=2,'col'=2] {'row','col'}, dimensions={0}, use_global_device_ids=true | all-gather | bytes 122880 | tf_op jit(solution)/shard_map/all_gather | solution.py:24
  (476 shorter events, 458.9 us)
Async XLA Ops:
  1.6 18.9 %all-to-all-start.3 = ((bf16[4,2,16,1024]{3,2,1,0:T(8,128)(2,1)}), bf16[4,2,16,1024]{3,2,1,0:T(8,128)(2,1)S(1)}, u32[]{:S(2)}, u32[]{:S(2)}) async-start(bf16[4,2,16,1024]{3,2,1,0:T(8,128)(2,1)} %stack.15), calls=%async_computation.3 | async-start | bytes 524288 | tf_op jit(solution)/shard_map/all_to_all | solution.py:59
  48.0 12.5 %all-to-all-start = ((bf16[4,2,16,1024]{3,2,1,0:T(8,128)(2,1)}), bf16[4,2,16,1024]{3,2,1,0:T(8,128)(2,1)S(1)}, u32[]{:S(2)}, u32[]{:S(2)}) async-start(bf16[4,2,16,1024]{3,2,1,0:T(8,128)(2,1)} %stack.18), calls=%async_computation | async-start | bytes 524288 | tf_op jit(solution)/shard_map/while/body/eval_jaxpr/all_to_all | solution.py:59
  76.6 11.0 %all-to-all-start.2 = ((f32[4,1,6656]{2,1,0:T(1,128)}), f32[4,1,6656]{2,1,0:T(1,128)S(1)}, u32[]{:S(2)}, u32[]{:S(2)}) async-start(f32[4,1,6656]{2,1,0:T(1,128)} %broadcast_in_dim.16), calls=%async_computation.2 | async-start | bytes 212992 | tf_op jit(solution)/shard_map/while/body/eval_jaxpr/all_to_all | solution.py:29
  97.6 13.4 %all-to-all-start = ((bf16[4,2,16,1024]{3,2,1,0:T(8,128)(2,1)}), bf16[4,2,16,1024]{3,2,1,0:T(8,128)(2,1)S(1)}, u32[]{:S(2)}, u32[]{:S(2)}) async-start(bf16[4,2,16,1024]{3,2,1,0:T(8,128)(2,1)} %stack.18), calls=%async_computation | async-start | bytes 524288 | tf_op jit(solution)/shard_map/while/body/eval_jaxpr/all_to_all | solution.py:59
  127.0 11.0 %all-to-all-start.2 = ((f32[4,1,6656]{2,1,0:T(1,128)}), f32[4,1,6656]{2,1,0:T(1,128)S(1)}, u32[]{:S(2)}, u32[]{:S(2)}) async-start(f32[4,1,6656]{2,1,0:T(1,128)} %broadcast_in_dim.16), calls=%async_computation.2 | async-start | bytes 212992 | tf_op jit(solution)/shard_map/while/body/eval_jaxpr/all_to_all | solution.py:29
  147.9 13.4 %all-to-all-start = ((bf16[4,2,16,1024]{3,2,1,0:T(8,128)(2,1)}), bf16[4,2,16,1024]{3,2,1,0:T(8,128)(2,1)S(1)}, u32[]{:S(2)}, u32[]{:S(2)}) async-start(bf16[4,2,16,1024]{3,2,1,0:T(8,128)(2,1)} %stack.18), calls=%async_computation | async-start | bytes 524288 | tf_op jit(solution)/shard_map/while/body/eval_jaxpr/all_to_all | solution.py:59
  177.4 11.0 %all-to-all-start.2 = ((f32[4,1,6656]{2,1,0:T(1,128)}), f32[4,1,6656]{2,1,0:T(1,128)S(1)}, u32[]{:S(2)}, u32[]{:S(2)}) async-start(f32[4,1,6656]{2,1,0:T(1,128)} %broadcast_in_dim.16), calls=%async_computation.2 | async-start | bytes 212992 | tf_op jit(solution)/shard_map/while/body/eval_jaxpr/all_to_all | solution.py:29
  198.3 13.4 %all-to-all-start = ((bf16[4,2,16,1024]{3,2,1,0:T(8,128)(2,1)}), bf16[4,2,16,1024]{3,2,1,0:T(8,128)(2,1)S(1)}, u32[]{:S(2)}, u32[]{:S(2)}) async-start(bf16[4,2,16,1024]{3,2,1,0:T(8,128)(2,1)} %stack.18), calls=%async_computation | async-start | bytes 524288 | tf_op jit(solution)/shard_map/while/body/eval_jaxpr/all_to_all | solution.py:59
  227.7 11.0 %all-to-all-start.2 = ((f32[4,1,6656]{2,1,0:T(1,128)}), f32[4,1,6656]{2,1,0:T(1,128)S(1)}, u32[]{:S(2)}, u32[]{:S(2)}) async-start(f32[4,1,6656]{2,1,0:T(1,128)} %broadcast_in_dim.16), calls=%async_computation.2 | async-start | bytes 212992 | tf_op jit(solution)/shard_map/while/body/eval_jaxpr/all_to_all | solution.py:29
  248.7 13.4 %all-to-all-start = ((bf16[4,2,16,1024]{3,2,1,0:T(8,128)(2,1)}), bf16[4,2,16,1024]{3,2,1,0:T(8,128)(2,1)S(1)}, u32[]{:S(2)}, u32[]{:S(2)}) async-start(bf16[4,2,16,1024]{3,2,1,0:T(8,128)(2,1)} %stack.18), calls=%async_computation | async-start | bytes 524288 | tf_op jit(solution)/shard_map/while/body/eval_jaxpr/all_to_all | solution.py:59
  278.1 11.0 %all-to-all-start.2 = ((f32[4,1,6656]{2,1,0:T(1,128)}), f32[4,1,6656]{2,1,0:T(1,128)S(1)}, u32[]{:S(2)}, u32[]{:S(2)}) async-start(f32[4,1,6656]{2,1,0:T(1,128)} %broadcast_in_dim.16), calls=%async_computation.2 | async-start | bytes 212992 | tf_op jit(solution)/shard_map/while/body/eval_jaxpr/all_to_all | solution.py:29
  299.0 13.4 %all-to-all-start = ((bf16[4,2,16,1024]{3,2,1,0:T(8,128)(2,1)}), bf16[4,2,16,1024]{3,2,1,0:T(8,128)(2,1)S(1)}, u32[]{:S(2)}, u32[]{:S(2)}) async-start(bf16[4,2,16,1024]{3,2,1,0:T(8,128)(2,1)} %stack.18), calls=%async_computation | async-start | bytes 524288 | tf_op jit(solution)/shard_map/while/body/eval_jaxpr/all_to_all | solution.py:59
  328.5 11.0 %all-to-all-start.2 = ((f32[4,1,6656]{2,1,0:T(1,128)}), f32[4,1,6656]{2,1,0:T(1,128)S(1)}, u32[]{:S(2)}, u32[]{:S(2)}) async-start(f32[4,1,6656]{2,1,0:T(1,128)} %broadcast_in_dim.16), calls=%async_computation.2 | async-start | bytes 212992 | tf_op jit(solution)/shard_map/while/body/eval_jaxpr/all_to_all | solution.py:29
  349.4 13.4 %all-to-all-start = ((bf16[4,2,16,1024]{3,2,1,0:T(8,128)(2,1)}), bf16[4,2,16,1024]{3,2,1,0:T(8,128)(2,1)S(1)}, u32[]{:S(2)}, u32[]{:S(2)}) async-start(bf16[4,2,16,1024]{3,2,1,0:T(8,128)(2,1)} %stack.18), calls=%async_computation | async-start | bytes 524288 | tf_op jit(solution)/shard_map/while/body/eval_jaxpr/all_to_all | solution.py:59
  378.8 11.0 %all-to-all-start.2 = ((f32[4,1,6656]{2,1,0:T(1,128)}), f32[4,1,6656]{2,1,0:T(1,128)S(1)}, u32[]{:S(2)}, u32[]{:S(2)}) async-start(f32[4,1,6656]{2,1,0:T(1,128)} %broadcast_in_dim.16), calls=%async_computation.2 | async-start | bytes 212992 | tf_op jit(solution)/shard_map/while/body/eval_jaxpr/all_to_all | solution.py:29
  399.8 13.4 %all-to-all-start = ((bf16[4,2,16,1024]{3,2,1,0:T(8,128)(2,1)}), bf16[4,2,16,1024]{3,2,1,0:T(8,128)(2,1)S(1)}, u32[]{:S(2)}, u32[]{:S(2)}) async-start(bf16[4,2,16,1024]{3,2,1,0:T(8,128)(2,1)} %stack.18), calls=%async_computation | async-start | bytes 524288 | tf_op jit(solution)/shard_map/while/body/eval_jaxpr/all_to_all | solution.py:59
  429.2 11.0 %all-to-all-start.2 = ((f32[4,1,6656]{2,1,0:T(1,128)}), f32[4,1,6656]{2,1,0:T(1,128)S(1)}, u32[]{:S(2)}, u32[]{:S(2)}) async-start(f32[4,1,6656]{2,1,0:T(1,128)} %broadcast_in_dim.16), calls=%async_computation.2 | async-start | bytes 212992 | tf_op jit(solution)/shard_map/while/body/eval_jaxpr/all_to_all | solution.py:29
  449.4 13.4 %all-to-all-start = ((bf16[4,2,16,1024]{3,2,1,0:T(8,128)(2,1)}), bf16[4,2,16,1024]{3,2,1,0:T(8,128)(2,1)S(1)}, u32[]{:S(2)}, u32[]{:S(2)}) async-start(bf16[4,2,16,1024]{3,2,1,0:T(8,128)(2,1)} %stack.18), calls=%async_computation | async-start | bytes 524288 | tf_op jit(solution)/shard_map/while/body/eval_jaxpr/all_to_all | solution.py:59
  478.9 11.0 %all-to-all-start.2 = ((f32[4,1,6656]{2,1,0:T(1,128)}), f32[4,1,6656]{2,1,0:T(1,128)S(1)}, u32[]{:S(2)}, u32[]{:S(2)}) async-start(f32[4,1,6656]{2,1,0:T(1,128)} %broadcast_in_dim.16), calls=%async_computation.2 | async-start | bytes 212992 | tf_op jit(solution)/shard_map/while/body/eval_jaxpr/all_to_all | solution.py:29
  499.6 13.4 %all-to-all-start = ((bf16[4,2,16,1024]{3,2,1,0:T(8,128)(2,1)}), bf16[4,2,16,1024]{3,2,1,0:T(8,128)(2,1)S(1)}, u32[]{:S(2)}, u32[]{:S(2)}) async-start(bf16[4,2,16,1024]{3,2,1,0:T(8,128)(2,1)} %stack.18), calls=%async_computation | async-start | bytes 524288 | tf_op jit(solution)/shard_map/while/body/eval_jaxpr/all_to_all | solution.py:59
  529.1 11.0 %all-to-all-start.2 = ((f32[4,1,6656]{2,1,0:T(1,128)}), f32[4,1,6656]{2,1,0:T(1,128)S(1)}, u32[]{:S(2)}, u32[]{:S(2)}) async-start(f32[4,1,6656]{2,1,0:T(1,128)} %broadcast_in_dim.16), calls=%async_computation.2 | async-start | bytes 212992 | tf_op jit(solution)/shard_map/while/body/eval_jaxpr/all_to_all | solution.py:29
  549.8 13.4 %all-to-all-start = ((bf16[4,2,16,1024]{3,2,1,0:T(8,128)(2,1)}), bf16[4,2,16,1024]{3,2,1,0:T(8,128)(2,1)S(1)}, u32[]{:S(2)}, u32[]{:S(2)}) async-start(bf16[4,2,16,1024]{3,2,1,0:T(8,128)(2,1)} %stack.18), calls=%async_computation | async-start | bytes 524288 | tf_op jit(solution)/shard_map/while/body/eval_jaxpr/all_to_all | solution.py:59
  579.3 11.0 %all-to-all-start.2 = ((f32[4,1,6656]{2,1,0:T(1,128)}), f32[4,1,6656]{2,1,0:T(1,128)S(1)}, u32[]{:S(2)}, u32[]{:S(2)}) async-start(f32[4,1,6656]{2,1,0:T(1,128)} %broadcast_in_dim.16), calls=%async_computation.2 | async-start | bytes 212992 | tf_op jit(solution)/shard_map/while/body/eval_jaxpr/all_to_all | solution.py:29
  600.0 13.4 %all-to-all-start.5 = ((bf16[4,2,16,1024]{3,2,1,0:T(8,128)(2,1)}), bf16[4,2,16,1024]{3,2,1,0:T(8,128)(2,1)S(1)}, u32[]{:S(2)}, u32[]{:S(2)}) async-start(bf16[4,2,16,1024]{3,2,1,0:T(8,128)(2,1)} %stack.16), calls=%async_computation.5 | async-start | bytes 524288 | tf_op jit(solution)/shard_map/all_to_all | solution.py:59
  (3 other events, 587.3 us)
